TPU v7x, 32 devices: a whole 2x2x4 slice. The times are simulated.
32 devices in a mesh: dp: 8 (over z, x), section: 4 (over y, core).
Axes of the slice: x: 2, y: 2, z: 4, core: 2. Of those that a mesh axis runs over, the one named last changes fastest.
Arguments:
- activations: bfloat16 [4, 16, 512, 4096], P('section', 'dp'), may hold values from -16 to 16
- out_grads: bfloat16 [4, 16, 512, 1024], P('section', 'dp'), may hold values from -16 to 16
- lengths: int32 [16], P('dp'), may hold values from 64 to 512, as said below
Outputs:
- mean_grad: bfloat16 [4, 4096, 1024], P('section', 'dp')
- norm_ratio: float32 [16], P('dp')
Inputs may be any that keep to these rules, and one draw needn't show every extreme that they name: Example e's first lengths[e] token slots are real, the rest padding; some example fills all 512 slots.
All inputs are finite; a program needn't handle non-finite values.
Results may differ from a plain program's by a relative error of at most 0.015.
Values may be sent and summed in bfloat16 or wider, within the bound.
A program may use at most 128 MiB of HBM per device.

v0:
```python
import math
import jax
import jax.numpy as jnp
from jax import lax
from jax.sharding import PartitionSpec as P


def entering(value, axis, combine, identity):
    peers, mine = (lax.axis_size(axis), lax.axis_index(axis))
    everything = lax.all_gather(value, axis)
    start = jnp.broadcast_to(jnp.asarray(identity, value.dtype), value.shape)

    def lap(k, before):
        at = peers - 1 - k
        reached = at > mine
        new = combine(before, everything[at])
        return jnp.where(reached, new, before)

    return lax.fori_loop(0, peers, lap, start)


def from_root(value, axis, source):
    kept = jnp.where(lax.axis_index(axis) == source, value, 0).astype(value.dtype)
    return lax.psum(kept, axis)


def add_norms(earlier, later):
    return earlier + later


def row_term(flat_acts, flat_scaled, layer_index):
    columns = flat_acts[layer_index]
    return lax.dot_general(
        columns,
        flat_scaled[layer_index],
        (((0,), (0,)), ((), ())),
        preferred_element_type=jnp.float32,
    )


def on_device(activations, out_grads, lengths):
    layer_count, example_count, seq_len, model_width = activations.shape
    key_width = out_grads.shape[3]
    total_layers = layer_count * lax.axis_size("section")
    clip_bound = 0.5 * math.sqrt(float(total_layers * seq_len * model_width * key_width))
    positions = lax.broadcasted_iota(jnp.int32, (example_count, seq_len), 1)
    token_keep = (positions < lengths[:, None]).astype(jnp.bfloat16)
    masked = out_grads * token_keep[None, :, :, None]
    act_gram = jnp.einsum(
        "lesd,letd->lest", activations, activations, preferred_element_type=jnp.float32
    )
    grad_gram = jnp.einsum("lesk,letk->lest", masked, masked, preferred_element_type=jnp.float32)
    own_norms = jnp.sum(act_gram * grad_gram, axis=(0, 2, 3))
    later_norms = entering(own_norms, "section", add_norms, jnp.zeros_like(own_norms))
    norm_total = from_root(later_norms + own_norms, "section", 0)
    norm_ratio = jnp.sqrt(norm_total) / clip_bound
    clip_factor = 1.0 / jnp.maximum(norm_ratio, 1.0)
    scaled = (clip_factor[None, :, None, None] * masked).astype(jnp.bfloat16)
    flat_acts = activations.reshape(layer_count, example_count * seq_len, model_width)
    flat_scaled = scaled.reshape(layer_count, example_count * seq_len, key_width)
    examples_all = lax.axis_size("dp") * example_count
    pieces = [
        lax.psum_scatter(
            row_term(flat_acts, flat_scaled, 0).astype(jnp.bfloat16),
            "dp",
            scatter_dimension=0,
            tiled=True,
        ).astype(jnp.float32)
    ]
    stacked = jnp.stack(pieces)
    mean_grad = (stacked / examples_all).astype(jnp.bfloat16)
    return (mean_grad, norm_ratio)


def solution(mesh):
    placed = (P("section", "dp", None, None), P("section", "dp", None, None), P("dp"))
    return jax.shard_map(
        on_device,
        mesh=mesh,
        in_specs=placed,
        out_specs=(P("section", "dp", None), P("dp")),
        check_vma=False,
    )
```

profile of v0, /device:TPU:0, one launch (start us, length us, event | category | flops | bytes accessed | tf_op | source)
XLA Modules:
  0.0 212.2 jit_solution(11250981878342010992)
XLA Ops:
  7.2 0.0 reduce-scatter.2.cloned.1.call-start
  7.2 0.7 compare_convert_fusion
  8.0 1.3 dynamic-slice
  10.0 3.6 %fusion.8 = f32[2,512,512]{2,1,0:T(8,128)S(1)} fusion(bf16[1,2,512,1024]{3,2,1,0:T(8,128)(2,1)} %param.6, bf16[2,512]{1,0:T(2,128)(2,1)S(1)} %compare_convert_fusion), kind=kOutput, calls=%fused_computation.9 | convolution fusion | flops 1074790400 | bytes 4196352 | tf_op jit(solution)/shard_map/lesk,letk->lest/dot_general | solution.py:52
  13.6 0.0 copy-start
  13.6 10.7 %multiply_reduce_fusion = f32[2]{0:T(128)S(1)} fusion(f32[2,512,512]{2,1,0:T(8,128)S(1)} %fusion.8, bf16[1,2,512,4096]{3,2,1,0:T(8,128)(2,1)} %param.5), kind=kOutput, calls=%fused_computation.13 | convolution fusion | flops 4296015872 | bytes 10485768 | tf_op jit(solution)/shard_map/lesd,letd->lest/dot_general | solution.py:49
  24.3 0.2 dynamic-update-slice
  24.5 8.4 %all-reduce = f32[8]{0:T(128)S(1)} all-reduce(f32[8]{0:T(128)S(1)} %dynamic-update-slice), channel_id=2, replica_groups=mesh['dp'=8,'section'=4] {'section'}, use_global_device_ids=true, to_apply=%add | all-reduce | flops 8 | bytes 64
  32.8 0.1 reshape.49
  32.9 0.1 while.16
  33.1 5.8 %psum.7 = f32[2]{0:T(128)S(1)} all-reduce(f32[2]{0:T(128)S(1)} %broadcast_select_fusion.2), channel_id=1, replica_groups=mesh['dp'=8,'section'=4] {'section'}, use_global_device_ids=true, to_apply=%region_3.4 | all-reduce | flops 2 | bytes 16 | tf_op jit(solution)/shard_map/psum | solution.py:24
  38.9 0.5 maximum_divide_fusion
  39.4 0.0 copy-done
  39.4 14.9 %fusion.3 = bf16[4096,1024]{0,1:T(8,128)(2,1)} fusion(bf16[1,2,512,4096]{3,2,1,0:T(8,128)(2,1)} %param.5, f32[2]{0:T(128)S(1)} %get-tuple-element.140, bf16[1,2,512,1024]{3,2,1,0:T(8,128)(2,1)S(1)} %copy-done, bf16[2,512]{1,0:T(2,128)(2,1)S(1)} %compare_convert_fusion), kind=kOutput, calls=%fused_computation.6 | convolution fusion | flops 8598323200 | bytes 18876424 | tf_op jit(solution)/shard_map/dot_general | solution.py:33
  54.3 0.0 reduce-scatter.2.cloned.1.call-update
  54.3 148.4 %reduce-scatter.2.cloned.1.call-done = bf16[512,1024]{0,1:T(8,128)(2,1)} async-done(((bf16[4096,1024]{0,1:T(8,128)(2,1)}), bf16[512,1024]{0,1:T(8,128)(2,1)}) %reduce-scatter.2.cloned.1.call-update) | async-done | bytes 1048592 | tf_op jit(solution)/shard_map/reduce_scatter | solution.py:63
  202.7 1.4 fusion.15
  204.1 1.3 copy.8
  (7 shorter events, 0.1 us)
Async XLA Ops:
  7.2 195.5 %reduce-scatter.2.cloned.1.call-start = ((), (), s32[]{:S(2)}) async-start(), calls=%async_computation.1 | async-start | bytes 9437184 | tf_op jit(solution)/shard_map/reduce_scatter | solution.py:63
  13.6 25.8 %copy-start = (bf16[1,2,512,1024]{3,2,1,0:T(8,128)(2,1)S(1)}, bf16[1,2,512,1024]{3,2,1,0:T(8,128)(2,1)}, u32[]{:S(2)}) copy-start(bf16[1,2,512,1024]{3,2,1,0:T(8,128)(2,1)} %param.6) | copy-start | bytes 6291460
Sparse Core Ops, SparseCore 0:
  54.4 148.2 reduce-scatter.1
where the time goes:
time: 213 us; the launch traced here: 212 us
  waiting for transfers between devices  148 us (69%)
  matrix products  29.1 us (14%)
  between operations  14.8 us (7%)
  blocking collectives  14.1 us (7%)
  local copies, waits for them, and re-layouts  2.91 us (1%)
  other arithmetic  2.74 us (1%)
    reduce_scatter x1, waiting for transfers between devices, on_device(): lax.psum_scatter(row_term(flat_acts, flat_scaled, 0).astype(jnp.bfloat16)...  148 us
    dot_general x1, matrix products, row_term(): lax.dot_general(columns, flat_scaled[layer_index], (((0,), (0,)), ((), ()...  14.9 us
    dot_general x1, matrix products, on_device(): jnp.einsum('lesd,letd->lest', activations, activations, preferred_element...  10.7 us
    unnamed x1, blocking collectives  8.38 us
    psum x1, blocking collectives, from_root(): return lax.psum(kept, axis)  5.76 us
  transfers between devices with their start and end apart: 1, of which 1 were waited for; matrix products, arithmetic and copies ran while one was open for 0% of the time, Pallas kernels for 0%

commit v1 on v0

--- a/solution.py
+++ b/solution.py
@@ -21,7 +21,7 @@
 
 def from_root(value, axis, source):
     kept = jnp.where(lax.axis_index(axis) == source, value, 0).astype(value.dtype)
-    return lax.psum(kept, axis)
+    return jnp.sum(lax.all_gather(kept, axis), axis=0)
 
 
 def add_norms(earlier, later):

time: 213 us -> 213 us (level)
    psum x1 -> x0, blocking collectives: 5.76 us -> none  [from_root(): return lax.psum(kept, axis)]
    unnamed x1 -> x2, blocking collectives: 8.38 us -> 14.1 us
where the time goes in v1:
time: 213 us; the launch traced here: 212 us
  waiting for transfers between devices  148 us (69%)
  matrix products  29.1 us (14%)
  between operations  14.7 us (7%)
  blocking collectives  14.1 us (7%)
  local copies, waits for them, and re-layouts  2.92 us (1%)
  other arithmetic  2.86 us (1%)
    reduce_scatter x1, waiting for transfers between devices, on_device(): lax.psum_scatter(row_term(flat_acts, flat_scaled, 0).astype(jnp.bfloat16)...  148 us
    dot_general x1, matrix products, row_term(): lax.dot_general(columns, flat_scaled[layer_index], (((0,), (0,)), ((), ()...  14.9 us
    unnamed x2, blocking collectives  14.1 us
    dot_general x1, matrix products, on_device(): jnp.einsum('lesd,letd->lest', activations, activations, preferred_element...  10.7 us
  transfers between devices with their start and end apart: 1, of which 1 were waited for; matrix products, arithmetic and copies ran while one was open for 0% of the time, Pallas kernels for 0%

profile of v1, /device:TPU:0, one launch (start us, length us, event | category | flops | bytes accessed | tf_op | source)
XLA Modules:
  0.0 212.3 jit_solution(10347858545942672140)
XLA Ops:
  7.2 0.0 reduce-scatter.2.cloned.1.call-start
  7.2 0.7 compare_convert_fusion
  8.0 1.2 dynamic-slice
  9.9 3.6 %fusion.8 = f32[2,512,512]{2,1,0:T(8,128)S(1)} fusion(bf16[1,2,512,1024]{3,2,1,0:T(8,128)(2,1)} %param.6, bf16[2,512]{1,0:T(2,128)(2,1)S(1)} %compare_convert_fusion), kind=kOutput, calls=%fused_computation.9 | convolution fusion | flops 1074790400 | bytes 4196352 | tf_op jit(solution)/shard_map/lesk,letk->lest/dot_general | solution.py:52
  13.4 0.0 copy-start
  13.5 10.7 %multiply_reduce_fusion = f32[2]{0:T(128)S(1)} fusion(f32[2,512,512]{2,1,0:T(8,128)S(1)} %fusion.8, bf16[1,2,512,4096]{3,2,1,0:T(8,128)(2,1)} %param.5), kind=kOutput, calls=%fused_computation.13 | convolution fusion | flops 4296015872 | bytes 10485768 | tf_op jit(solution)/shard_map/lesd,letd->lest/dot_general | solution.py:49
  24.1 0.2 dynamic-update-slice
  24.3 8.4 %all-reduce = f32[8]{0:T(128)S(1)} all-reduce(f32[8]{0:T(128)S(1)} %dynamic-update-slice), channel_id=2, replica_groups=mesh['dp'=8,'section'=4] {'section'}, use_global_device_ids=true, to_apply=%add | all-reduce | flops 8 | bytes 64
  32.7 0.1 reshape.54
  32.8 0.1 while.16
  32.9 0.1 fusion.18
  33.0 5.7 %all-reduce.1 = f32[8]{0:T(128)S(1)} all-reduce(f32[8]{0:T(128)S(1)} %fusion.18), channel_id=3, replica_groups=mesh['dp'=8,'section'=4] {'section'}, use_global_device_ids=true, to_apply=%add.1 | all-reduce | flops 8 | bytes 64
  38.8 0.1 reshape.55
  38.9 0.5 maximum_divide_fusion
  39.4 0.0 copy-done
  39.4 14.9 %fusion.3 = bf16[4096,1024]{0,1:T(8,128)(2,1)} fusion(bf16[1,2,512,4096]{3,2,1,0:T(8,128)(2,1)} %param.5, f32[2]{0:T(128)S(1)} %get-tuple-element.140, bf16[1,2,512,1024]{3,2,1,0:T(8,128)(2,1)S(1)} %copy-done, bf16[2,512]{1,0:T(2,128)(2,1)S(1)} %compare_convert_fusion), kind=kOutput, calls=%fused_computation.6 | convolution fusion | flops 8598323200 | bytes 18876424 | tf_op jit(solution)/shard_map/dot_general | solution.py:33
  54.3 0.0 reduce-scatter.2.cloned.1.call-update
  54.3 148.4 %reduce-scatter.2.cloned.1.call-done = bf16[512,1024]{0,1:T(8,128)(2,1)} async-done(((bf16[4096,1024]{0,1:T(8,128)(2,1)}), bf16[512,1024]{0,1:T(8,128)(2,1)}) %reduce-scatter.2.cloned.1.call-update) | async-done | bytes 1048592 | tf_op jit(solution)/shard_map/reduce_scatter | solution.py:63
  202.7 1.4 fusion.15
  204.1 1.3 copy.8
  (8 shorter events, 0.1 us)
Async XLA Ops:
  7.2 195.6 %reduce-scatter.2.cloned.1.call-start = ((), (), s32[]{:S(2)}) async-start(), calls=%async_computation.1 | async-start | bytes 9437184 | tf_op jit(solution)/shard_map/reduce_scatter | solution.py:63
  13.4 26.0 %copy-start = (bf16[1,2,512,1024]{3,2,1,0:T(8,128)(2,1)S(1)}, bf16[1,2,512,1024]{3,2,1,0:T(8,128)(2,1)}, u32[]{:S(2)}) copy-start(bf16[1,2,512,1024]{3,2,1,0:T(8,128)(2,1)} %param.6) | copy-start | bytes 6291460
Sparse Core Ops, SparseCore 0:
  54.4 148.2 reduce-scatter.1
